TPU v7x, 32 devices: a whole 2x2x4 slice. The times are simulated.
32 devices in a mesh: tok: 8 (over y, x, core), exp: 4 (over z).
Axes of the slice: x: 2, y: 2, z: 4, core: 2. Of those that a mesh axis runs over, the one named last changes fastest.
Arguments:
- expert_rows: bfloat16 [4, 2048, 4096], P('exp', 'tok'), may hold values from -480 to 480
- router_input: bfloat16 [2048, 4096], P(('tok', 'exp')), may hold values from -6 to 6
- router_weight: float32 [4096, 4], replicated, may hold values from -0.09375 to 0.09375
- assign: int32 [2048, 2], P(('tok', 'exp')), may hold values from 0 to 3, all different within a row
- targets: int32 [2048], P(('tok', 'exp')), may hold values from 0 to 15999
- head: bfloat16 [4096, 16000], P('tok', 'exp'), may hold values from -0.35 to 0.35
Outputs:
- token_loss: float32 [2048], P(('tok', 'exp'))
- router_grad: float32 [4096, 4], replicated
- mean_loss: float32 [], replicated
All inputs are finite; a program needn't handle non-finite values.
Results may differ from a plain program's by a relative error of at most 0.007.
Values may be sent and summed in bfloat16 or wider, within the bound.
A program may use at most 128 MiB of HBM per device.

v0:
```python
import math
import jax
import jax.numpy as jnp
from jax import lax
from jax.sharding import PartitionSpec as P


def shards(expert_rows, router_input, router_weight, assign, targets, head):
    experts = router_weight.shape[1]
    own_rows = router_input.shape[0]
    tokens_all = own_rows * lax.axis_size("tok") * lax.axis_size("exp")
    loss_scale = 1.0 / math.sqrt(tokens_all)
    inputs = router_input.astype(jnp.float32)
    gate_logits = jnp.dot(inputs, router_weight, precision=lax.Precision.HIGHEST)
    labels = jnp.arange(experts, dtype=jnp.int32)
    first_hot = (assign[:, 0:1] == labels[None, :]).astype(jnp.float32)
    second_hot = (assign[:, 1:2] == labels[None, :]).astype(jnp.float32)
    differ = first_hot - second_hot
    mix_share = jax.nn.sigmoid(jnp.sum(gate_logits * differ, axis=1))
    mixing = mix_share[:, None] * first_hot + (1.0 - mix_share)[:, None] * second_hot
    local_rows = lax.all_to_all(expert_rows, "exp", split_axis=1, concat_axis=0, tiled=True)
    local_wide = local_rows.astype(jnp.float32)
    mixed_own = jnp.sum(mixing.T[:, :, None] * local_wide, axis=0).astype(jnp.bfloat16)
    mixed_rows, group_targets = (
        lax.all_gather(mixed_own, "exp", axis=0, tiled=True),
        lax.all_gather(targets, "exp", axis=0, tiled=True),
    )
    shard_width = head.shape[1]
    full_head = lax.all_gather(head, "tok", axis=0, tiled=True)
    logits = jnp.dot(mixed_rows, full_head, preferred_element_type=jnp.float32)
    first_col = lax.axis_index("exp") * shard_width
    columns = first_col + jnp.arange(shard_width, dtype=jnp.int32)
    target_hit = group_targets[:, None] == columns[None, :]
    picked = jnp.sum(jnp.where(target_hit, logits, 0.0), axis=1)
    local_top = jnp.max(logits, axis=1)
    row_top = lax.pmax(local_top, "exp")
    exp_total, target_logit = lax.psum(
        (jnp.sum(jnp.exp(logits - row_top[:, None]), axis=1), picked), "exp"
    )
    log_total = row_top + jnp.log(exp_total)
    group_loss = log_total - target_logit
    own_loss = lax.dynamic_slice_in_dim(group_loss, lax.axis_index("exp") * own_rows, own_rows, 0)
    loss_sum = lax.psum(jnp.sum(own_loss), ("tok", "exp"))
    slope = (
        loss_scale * (jnp.exp(logits - log_total[:, None]) - target_hit.astype(jnp.float32))
    ).astype(jnp.bfloat16)
    hidden_slope = lax.psum_scatter(
        lax.dot_general(
            slope, full_head, (((1,), (1,)), ((), ())), preferred_element_type=jnp.float32
        ).astype(jnp.bfloat16),
        "exp",
        scatter_dimension=0,
        tiled=True,
    ).astype(jnp.float32)
    weight_slope = jnp.sum(hidden_slope[None, :, :] * local_wide, axis=2).T
    spread = jnp.sum(weight_slope * differ, axis=1) * mix_share * (1.0 - mix_share)
    gate_slope = spread[:, None] * differ
    router_part = jnp.dot(inputs.T, gate_slope, precision=lax.Precision.HIGHEST)
    router_sum = lax.psum(router_part, ("tok", "exp"))
    mean_loss = loss_sum / tokens_all
    return (own_loss, router_sum, mean_loss)


def solution(mesh):
    in_specs = (
        P("exp", "tok", None),
        P(("tok", "exp"), None),
        P(),
        P(("tok", "exp"), None),
        P(("tok", "exp")),
        P("tok", "exp"),
    )
    out_specs = (P(("tok", "exp")), P(), P())
    return jax.shard_map(shards, mesh=mesh, in_specs=in_specs, out_specs=out_specs, check_vma=False)
```

profile of v0, /device:TPU:1, one launch (start us, length us, event | category | flops | bytes accessed | tf_op | source)
XLA Modules:
  0.0 542.0 jit_solution(5459968139769704115)
XLA Ops:
  7.2 0.0 copy-start
  7.2 8.4 %copy.16 = bf16[1,256,4096]{2,0,1:T(2,128)(2,1)} copy(bf16[1,256,4096]{2,1,0:T(8,128)(2,1)} %param.6) | data formatting | bytes 4194304 | tf_op args[0]
  15.6 0.5 broadcast.107
  16.1 13.5 %reduce.1 = bf16[256,4096]{1,0:T(8,128)(2,1)S(1)} reduce(bf16[256,1,4096]{2,1,0:T(2,128)(2,1)} %bitcast.29, bf16[]{:T(256)} %broadcast.107), dimensions={1}, to_apply=%bitcast.25.reduce_sub_computation | reduce | bytes 4194306
  29.6 0.0 copy-start.3
  29.6 0.0 copy-start.2
  29.6 2.8 reshape.110
  32.4 5.4 all-to-all-start
  37.8 0.0 all-gather.3.cloned.1.call-start
  37.8 0.0 copy-done.3
  37.8 0.0 copy-done
  37.8 0.0 copy-done.2
  37.9 0.5 fusion.10
  38.4 47.2 %all-to-all-done = bf16[4,2,131072]{2,1,0:T(2,128)(2,1)S(1)} async-done(((bf16[4,2,131072]{2,1,0:T(2,128)(2,1)}), bf16[4,2,131072]{2,1,0:T(2,128)(2,1)S(1)}, u32[]{:S(2)}, u32[]{:S(2)}) %all-to-all-start) | async-done | bytes 2097184 | tf_op jit(solution)/shard_map/all_to_all | solution.py:21
  85.6 3.3 reshape.111
  88.9 6.0 %copy_convert_fusion = f32[1,256,4096]{2,1,0:T(8,128)S(1)} fusion(bf16[1,256,4096]{2,0,1:T(2,128)(2,1)} %bitcast.27), kind=kLoop, calls=%fused_computation.12 | loop fusion | flops 1048576 | bytes 6291456 | tf_op jit(solution)/shard_map/convert_element_type | solution.py:22
  94.9 0.0 copy-start.5
  94.9 0.0 copy-start.4
  94.9 1.4 multiply_reduce_fusion
  96.3 0.0 all-gather.3.cloned.1.call-update
  96.3 0.0 all-gather.5.cloned.1.call-start
  96.3 0.7 all-gather.5.cloned.1.call-update
  97.1 0.2 reduce-scatter.2.cloned.1.call-start
  97.3 0.0 copy-done.5
  97.3 0.6 dynamic-slice
  98.5 0.0 copy-done.4
  98.6 0.2 dynamic-update-slice
  98.8 4.0 all-reduce
  102.8 39.0 %all-gather.3.cloned.1.call-done = bf16[256,4096]{1,0:T(8,128)(2,1)} async-done(((bf16[64,4096]{1,0:T(8,128)(2,1)}), bf16[256,4096]{1,0:T(8,128)(2,1)}) %all-gather.3.cloned.1.call-update) | async-done | bytes 2097168 | tf_op jit(solution)/shard_map/all_gather | solution.py:25
  141.8 165.1 %all-gather.5.cloned.1.call-done = bf16[4096,4000]{0,1:T(8,128)(2,1)} async-done(((bf16[512,4000]{0,1:T(8,128)(2,1)}), bf16[4096,4000]{0,1:T(8,128)(2,1)}) %all-gather.5.cloned.1.call-update) | async-done | bytes 32768016 | tf_op jit(solution)/shard_map/all_gather | solution.py:29
  306.9 16.2 %fusion.19 = (f32[256]{0:T(256)S(1)}, f32[256,4000]{0,1:T(8,128)}) fusion(bf16[256,4096]{1,0:T(8,128)(2,1)} %all-gather.3.cloned.1.call-done, bf16[4096,4000]{0,1:T(8,128)(2,1)} %all-gather.5.cloned.1.call-done), kind=kOutput, calls=%fused_computation.41 | convolution fusion | flops 8389632000 | bytes 38962176 | tf_op jit(solution)/shard_map/dot_general | solution.py:30
  323.2 9.7 %pmax.7 = f32[256]{0:T(256)S(1)} all-reduce(f32[256]{0:T(256)S(1)} %get-tuple-element.15), channel_id=1, replica_groups=mesh['tok'=8,'exp'=4] {'exp'}, use_global_device_ids=true, to_apply=%region_3.4 | all-reduce | flops 256 | bytes 2048 | tf_op jit(solution)/shard_map/pmax | solution.py:36
  332.8 3.9 fusion.1
  336.7 6.6 %all-reduce.1 = (f32[256]{0:T(256)S(1)}, f32[256]{0:T(256)S(1)}) all-reduce(f32[256]{0:T(256)S(1)} %get-tuple-element.4, f32[256]{0:T(256)S(1)} %get-tuple-element.3), channel_id=1, replica_groups=mesh['tok'=8,'exp'=4] {'exp'}, use_global_device_ids=true, to_apply=%region_5.6 | all-reduce | flops 512 | bytes 4096 | tf_op jit(solution)/shard_map/psum | solution.py:37
  343.3 17.2 %convolution_convert_fusion = bf16[256,4096]{1,0:T(8,128)(2,1)} fusion(bf16[4096,4000]{0,1:T(8,128)(2,1)} %all-gather.5.cloned.1.call-done, f32[256,4000]{0,1:T(8,128)} %get-tuple-element.16, f32[256]{0:T(256)S(1)} %get-tuple-element.10, s32[256]{0:T(256)S(1)} %all-reduce, s32[4000]{0:T(1024)S(1)} %iota_add_fusion), kind=kOutput, calls=%fused_computation | convolution fusion | flops 8395800576 | bytes 38979200 | tf_op jit(solution)/shard_map/dot_general | solution.py:48
  360.5 0.0 reduce-scatter.2.cloned.1.call-update
  360.5 0.0 all-reduce.4.cloned.1.call-start
  360.6 45.4 %reduce-scatter.2.cloned.1.call-done = bf16[64,4096]{1,0:T(8,128)(2,1)} async-done(((bf16[256,4096]{1,0:T(8,128)(2,1)}), bf16[64,4096]{1,0:T(8,128)(2,1)}) %reduce-scatter.2.cloned.1.call-update) | async-done | bytes 524304 | tf_op jit(solution)/shard_map/reduce_scatter | solution.py:47
  406.0 0.0 copy-start.1
  406.0 1.7 mul.89
  407.6 0.7 copy-done.1
  408.3 2.4 fusion
  410.7 0.1 reduce_sum.70
  410.8 1.0 convolution_bitcast_fusion
  411.8 0.0 all-reduce.4.cloned.1.call-update
  411.8 1.2 fusion.17
  413.0 39.8 %psum.31 = f32[]{:T(128)} all-reduce(f32[]{:T(128)} %get-tuple-element.7), channel_id=1, replica_groups=mesh['tok'=8,'exp'=4] {'tok','exp'}, use_global_device_ids=true, to_apply=%region_13.14 | all-reduce | flops 1 | bytes 8 | tf_op jit(solution)/shard_map/psum | solution.py:43
  453.4 79.5 %all-reduce.4.cloned.1.call-done = f32[4096,4]{0,1:T(4,128)} async-done(((f32[4096,4]{0,1:T(4,128)}), f32[4096,4]{0,1:T(4,128)}) %all-reduce.4.cloned.1.call-update) | async-done | bytes 65552 | tf_op jit(solution)/shard_map/psum | solution.py:59
  532.9 1.5 copy.19
  (8 shorter events, 0.1 us)
Async XLA Ops:
  7.2 30.7 %copy-start = (bf16[64,4096]{1,0:T(8,128)(2,1)S(1)}, bf16[64,4096]{1,0:T(8,128)(2,1)}, u32[]{:S(2)}) copy-start(bf16[64,4096]{1,0:T(8,128)(2,1)} %param.7) | copy-start | bytes 1572868
  29.6 8.2 %copy-start.3 = (s32[64,2]{0,1:T(2,128)S(1)}, s32[64,2]{0,1:T(2,128)}, u32[]{:S(2)}) copy-start(s32[64,2]{0,1:T(2,128)} %param.9) | copy-start | bytes 1540
  29.6 8.2 %copy-start.2 = (f32[4096,4]{0,1:T(4,128)S(1)}, f32[4096,4]{0,1:T(4,128)}, u32[]{:S(2)}) copy-start(f32[4096,4]{0,1:T(4,128)} %param.8) | copy-start | bytes 196612
  32.4 53.2 %all-to-all-start = ((bf16[4,2,131072]{2,1,0:T(2,128)(2,1)}), bf16[4,2,131072]{2,1,0:T(2,128)(2,1)S(1)}, u32[]{:S(2)}, u32[]{:S(2)}) async-start(bf16[4,2,131072]{2,1,0:T(2,128)(2,1)} %reshape.110), calls=%async_computation | async-start | bytes 4194304 | tf_op jit(solution)/shard_map/all_to_all | solution.py:21
  37.8 104.0 %all-gather.3.cloned.1.call-start = ((), (), s32[]{:S(2)}) async-start(), calls=%async_computation.2 | async-start | bytes 2621440 | tf_op jit(solution)/shard_map/all_gather | solution.py:25
  94.9 2.4 copy-start.5
  94.9 3.6 copy-start.4
  96.3 210.6 %all-gather.5.cloned.1.call-start = ((), (), s32[]{:S(2)}) async-start(), calls=%async_computation.3 | async-start | bytes 36864000 | tf_op jit(solution)/shard_map/all_gather | solution.py:29
  97.1 308.9 %reduce-scatter.2.cloned.1.call-start = ((), (), s32[]{:S(2)}) async-start(), calls=%async_computation.4 | async-start | bytes 2621440 | tf_op jit(solution)/shard_map/reduce_scatter | solution.py:47
  360.5 172.3 %all-reduce.4.cloned.1.call-start = ((), (), s32[]{:S(2)}) async-start(), calls=%async_computation.5 | async-start | bytes 131072 | tf_op jit(solution)/shard_map/psum | solution.py:59
  406.0 2.3 copy-start.1
Sparse Core Ops, SparseCore 0:
  96.4 45.3 all-gather.2
  143.6 163.2 all-gather.4
  360.7 45.2 reduce-scatter.1
  412.0 120.8 all-reduce.3
where the time goes:
time: 543 us; the launch traced here: 542 us
  waiting for transfers between devices  377 us (69%)
  blocking collectives  60.1 us (11%)
  matrix products  34.9 us (6%)
  other arithmetic  28.4 us (5%)
  local copies, waits for them, and re-layouts  19.7 us (4%)
  between operations  16.3 us (3%)
  starting transfers between devices  5.71 us (1%)
    all_gather x1, waiting for transfers between devices, shards(): full_head = lax.all_gather(head, 'tok', axis=0, tiled=True)  165 us
    psum x1, waiting for transfers between devices, shards(): router_sum = lax.psum(router_part, ('tok', 'exp'))  79.5 us
    all_to_all x1, waiting for transfers between devices, shards(): lax.all_to_all(expert_rows, 'exp', split_axis=1, concat_axis=0, tiled=True)  47.2 us
    reduce_scatter x1, waiting for transfers between devices, shards(): lax.psum_scatter(lax.dot_general(slope, full_head, (((1,), (1,)), ((), ()...  45.4 us
    psum x1, blocking collectives, shards(): loss_sum = lax.psum(jnp.sum(own_loss), ('tok', 'exp'))  39.8 us
    all_gather x1, waiting for transfers between devices, shards(): lax.all_gather(mixed_own, 'exp', axis=0, tiled=True)  39 us
    unnamed x20, local copies, waits for them, and re-layouts  18 us
    dot_general x1, matrix products, shards(): lax.dot_general(slope, full_head, (((1,), (1,)), ((), ())), preferred_ele...  17.2 us
  transfers between devices with their start and end apart: 5, of which 5 were waited for; matrix products, arithmetic and copies ran while one was open for 0% of the time, Pallas kernels for 0%

commit v1 on v0

--- a/solution.py
+++ b/solution.py
@@ -56,7 +56,8 @@
     spread = jnp.sum(weight_slope * differ, axis=1) * mix_share * (1.0 - mix_share)
     gate_slope = spread[:, None] * differ
     router_part = jnp.dot(inputs.T, gate_slope, precision=lax.Precision.HIGHEST)
-    router_sum = lax.psum(router_part, ("tok", "exp"))
+    place_pipes = lambda chunk: lax.psum(lax.psum(chunk, axis_name="exp"), axis_name="tok")
+    router_sum = place_pipes(router_part)
     mean_loss = loss_sum / tokens_all
     return (own_loss, router_sum, mean_loss)
 

time: 543 us -> 512 us (0.943)
  waiting for transfers between devices: 377 us -> 343 us
    psum x1 -> x2, waiting for transfers between devices: 79.5 us -> 45.5 us  [the longest x1 32 us: shards(): lax.psum(chunk, axis_name='exp')]
  transfers between devices with their start and end apart: 5 -> 6, of which waited for: 5 -> 6; matrix products, arithmetic and copies ran while one was open for 0% -> 1% of each run, Pallas kernels for 0% -> 0%
where the time goes in v1:
time: 512 us; the launch traced here: 510 us
  waiting for transfers between devices  343 us (67%)
  blocking collectives  61.9 us (12%)
  matrix products  34.9 us (7%)
  other arithmetic  28.4 us (6%)
  local copies, waits for them, and re-layouts  19.7 us (4%)
  between operations  16.3 us (3%)
  starting transfers between devices  5.75 us (1%)
    all_gather x1, waiting for transfers between devices, shards(): full_head = lax.all_gather(head, 'tok', axis=0, tiled=True)  165 us
    all_to_all x1, waiting for transfers between devices, shards(): lax.all_to_all(expert_rows, 'exp', split_axis=1, concat_axis=0, tiled=True)  47.2 us
    reduce_scatter x1, waiting for transfers between devices, shards(): lax.psum_scatter(lax.dot_general(slope, full_head, (((1,), (1,)), ((), ()...  45.4 us
    psum x1, blocking collectives, shards(): loss_sum = lax.psum(jnp.sum(own_loss), ('tok', 'exp'))  41.6 us
    all_gather x1, waiting for transfers between devices, shards(): lax.all_gather(mixed_own, 'exp', axis=0, tiled=True)  39 us
    psum x1, waiting for transfers between devices, shards(): lax.psum(chunk, axis_name='exp')  32 us
    unnamed x20, local copies, waits for them, and re-layouts  18 us
    dot_general x1, matrix products, shards(): lax.dot_general(slope, full_head, (((1,), (1,)), ((), ())), preferred_ele...  17.2 us
  transfers between devices with their start and end apart: 6, of which 6 were waited for; matrix products, arithmetic and copies ran while one was open for 1% of the time, Pallas kernels for 0%

profile of v1, /device:TPU:1, one launch (start us, length us, event | category | flops | bytes accessed | tf_op | source)
XLA Modules:
  0.0 510.0 jit_solution(3449989466106876649)
XLA Ops:
  7.2 0.0 copy-start
  7.2 8.4 %copy.16 = bf16[1,256,4096]{2,0,1:T(2,128)(2,1)} copy(bf16[1,256,4096]{2,1,0:T(8,128)(2,1)} %param.6) | data formatting | bytes 4194304 | tf_op args[0]
  15.6 0.5 broadcast.107
  16.1 13.5 %reduce.1 = bf16[256,4096]{1,0:T(8,128)(2,1)S(1)} reduce(bf16[256,1,4096]{2,1,0:T(2,128)(2,1)} %bitcast.29, bf16[]{:T(256)} %broadcast.107), dimensions={1}, to_apply=%bitcast.25.reduce_sub_computation | reduce | bytes 4194306
  29.6 0.0 copy-start.3
  29.6 0.0 copy-start.2
  29.6 2.8 reshape.110
  32.4 5.4 %all-to-all-start = ((bf16[4,2,131072]{2,1,0:T(2,128)(2,1)}), bf16[4,2,131072]{2,1,0:T(2,128)(2,1)S(1)}, u32[]{:S(2)}, u32[]{:S(2)}) async-start(bf16[4,2,131072]{2,1,0:T(2,128)(2,1)} %reshape.110), calls=%async_computation | async-start | bytes 4194304 | tf_op jit(solution)/shard_map/all_to_all | solution.py:21
  37.8 0.0 all-gather.3.cloned.1.call-start
  37.8 0.0 copy-done.3
  37.8 0.0 copy-done
  37.8 0.0 copy-done.2
  37.9 0.5 fusion.10
  38.4 47.2 %all-to-all-done = bf16[4,2,131072]{2,1,0:T(2,128)(2,1)S(1)} async-done(((bf16[4,2,131072]{2,1,0:T(2,128)(2,1)}), bf16[4,2,131072]{2,1,0:T(2,128)(2,1)S(1)}, u32[]{:S(2)}, u32[]{:S(2)}) %all-to-all-start) | async-done | bytes 2097184 | tf_op jit(solution)/shard_map/all_to_all | solution.py:21
  85.6 3.3 reshape.111
  88.9 6.0 %copy_convert_fusion = f32[1,256,4096]{2,1,0:T(8,128)S(1)} fusion(bf16[1,256,4096]{2,0,1:T(2,128)(2,1)} %bitcast.27), kind=kLoop, calls=%fused_computation.12 | loop fusion | flops 1048576 | bytes 6291456 | tf_op jit(solution)/shard_map/convert_element_type | solution.py:22
  94.9 0.0 copy-start.5
  94.9 0.0 copy-start.4
  94.9 1.4 multiply_reduce_fusion
  96.3 0.0 all-gather.3.cloned.1.call-update
  96.3 0.0 all-gather.5.cloned.1.call-start
  96.3 0.7 all-gather.5.cloned.1.call-update
  97.1 0.2 reduce-scatter.2.cloned.1.call-start
  97.3 0.0 copy-done.5
  97.3 0.6 dynamic-slice
  98.5 0.0 copy-done.4
  98.6 0.2 dynamic-update-slice
  98.8 4.0 all-reduce
  102.8 39.0 %all-gather.3.cloned.1.call-done = bf16[256,4096]{1,0:T(8,128)(2,1)} async-done(((bf16[64,4096]{1,0:T(8,128)(2,1)}), bf16[256,4096]{1,0:T(8,128)(2,1)}) %all-gather.3.cloned.1.call-update) | async-done | bytes 2097168 | tf_op jit(solution)/shard_map/all_gather | solution.py:25
  141.8 165.1 %all-gather.5.cloned.1.call-done = bf16[4096,4000]{0,1:T(8,128)(2,1)} async-done(((bf16[512,4000]{0,1:T(8,128)(2,1)}), bf16[4096,4000]{0,1:T(8,128)(2,1)}) %all-gather.5.cloned.1.call-update) | async-done | bytes 32768016 | tf_op jit(solution)/shard_map/all_gather | solution.py:29
  306.9 16.2 %fusion.19 = (f32[256]{0:T(256)S(1)}, f32[256,4000]{0,1:T(8,128)}) fusion(bf16[256,4096]{1,0:T(8,128)(2,1)} %all-gather.3.cloned.1.call-done, bf16[4096,4000]{0,1:T(8,128)(2,1)} %all-gather.5.cloned.1.call-done), kind=kOutput, calls=%fused_computation.41 | convolution fusion | flops 8389632000 | bytes 38962176 | tf_op jit(solution)/shard_map/dot_general | solution.py:30
  323.2 9.7 %pmax.7 = f32[256]{0:T(256)S(1)} all-reduce(f32[256]{0:T(256)S(1)} %get-tuple-element.15), channel_id=1, replica_groups=mesh['tok'=8,'exp'=4] {'exp'}, use_global_device_ids=true, to_apply=%region_3.4 | all-reduce | flops 256 | bytes 2048 | tf_op jit(solution)/shard_map/pmax | solution.py:36
  332.8 3.9 fusion.1
  336.7 6.6 %all-reduce.1 = (f32[256]{0:T(256)S(1)}, f32[256]{0:T(256)S(1)}) all-reduce(f32[256]{0:T(256)S(1)} %get-tuple-element.4, f32[256]{0:T(256)S(1)} %get-tuple-element.3), channel_id=1, replica_groups=mesh['tok'=8,'exp'=4] {'exp'}, use_global_device_ids=true, to_apply=%region_5.6 | all-reduce | flops 512 | bytes 4096 | tf_op jit(solution)/shard_map/psum | solution.py:37
  343.3 17.2 %convolution_convert_fusion = bf16[256,4096]{1,0:T(8,128)(2,1)} fusion(bf16[4096,4000]{0,1:T(8,128)(2,1)} %all-gather.5.cloned.1.call-done, f32[256,4000]{0,1:T(8,128)} %get-tuple-element.16, f32[256]{0:T(256)S(1)} %get-tuple-element.10, s32[256]{0:T(256)S(1)} %all-reduce, s32[4000]{0:T(1024)S(1)} %iota_add_fusion), kind=kOutput, calls=%fused_computation | convolution fusion | flops 8395800576 | bytes 38979200 | tf_op jit(solution)/shard_map/dot_general | solution.py:48
  360.5 0.0 reduce-scatter.2.cloned.1.call-update
  360.5 0.0 all-reduce.5.cloned.1.call-start
  360.6 45.4 %reduce-scatter.2.cloned.1.call-done = bf16[64,4096]{1,0:T(8,128)(2,1)} async-done(((bf16[256,4096]{1,0:T(8,128)(2,1)}), bf16[64,4096]{1,0:T(8,128)(2,1)}) %reduce-scatter.2.cloned.1.call-update) | async-done | bytes 524304 | tf_op jit(solution)/shard_map/reduce_scatter | solution.py:47
  406.0 0.0 copy-start.1
  406.0 1.7 mul.89
  407.6 0.7 copy-done.1
  408.3 2.4 fusion
  410.7 0.1 reduce_sum.70
  410.8 1.0 convolution_bitcast_fusion
  411.8 0.0 all-reduce.5.cloned.1.call-update
  411.8 0.0 all-reduce.7.cloned.1.call-start
  411.8 32.0 %all-reduce.5.cloned.1.call-done = f32[4096,4]{0,1:T(4,128)} async-done(((f32[4096,4]{0,1:T(4,128)}), f32[4096,4]{0,1:T(4,128)}) %all-reduce.5.cloned.1.call-update) | async-done | bytes 65552 | tf_op jit(solution)/shard_map/psum | solution.py:59
  443.8 0.0 all-reduce.7.cloned.1.call-update
  443.8 1.2 fusion.17
  445.0 41.6 %psum.39 = f32[]{:T(128)} all-reduce(f32[]{:T(128)} %get-tuple-element.7), channel_id=1, replica_groups=mesh['tok'=8,'exp'=4] {'tok','exp'}, use_global_device_ids=true, to_apply=%region_14.15 | all-reduce | flops 1 | bytes 8 | tf_op jit(solution)/shard_map/psum | solution.py:43
  487.3 13.6 %all-reduce.7.cloned.1.call-done = f32[4096,4]{0,1:T(4,128)} async-done(((f32[4096,4]{0,1:T(4,128)}), f32[4096,4]{0,1:T(4,128)}) %all-reduce.7.cloned.1.call-update) | async-done | bytes 65552 | tf_op jit(solution)/shard_map/psum | solution.py:59
  500.9 1.5 copy.20
  (8 shorter events, 0.1 us)
Async XLA Ops:
  7.2 30.7 %copy-start = (bf16[64,4096]{1,0:T(8,128)(2,1)S(1)}, bf16[64,4096]{1,0:T(8,128)(2,1)}, u32[]{:S(2)}) copy-start(bf16[64,4096]{1,0:T(8,128)(2,1)} %param.7) | copy-start | bytes 1572868
  29.6 8.2 %copy-start.3 = (s32[64,2]{0,1:T(2,128)S(1)}, s32[64,2]{0,1:T(2,128)}, u32[]{:S(2)}) copy-start(s32[64,2]{0,1:T(2,128)} %param.9) | copy-start | bytes 1540
  29.6 8.2 %copy-start.2 = (f32[4096,4]{0,1:T(4,128)S(1)}, f32[4096,4]{0,1:T(4,128)}, u32[]{:S(2)}) copy-start(f32[4096,4]{0,1:T(4,128)} %param.8) | copy-start | bytes 196612
  32.4 53.2 %all-to-all-start = ((bf16[4,2,131072]{2,1,0:T(2,128)(2,1)}), bf16[4,2,131072]{2,1,0:T(2,128)(2,1)S(1)}, u32[]{:S(2)}, u32[]{:S(2)}) async-start(bf16[4,2,131072]{2,1,0:T(2,128)(2,1)} %reshape.110), calls=%async_computation | async-start | bytes 4194304 | tf_op jit(solution)/shard_map/all_to_all | solution.py:21
  37.8 104.0 %all-gather.3.cloned.1.call-start = ((), (), s32[]{:S(2)}) async-start(), calls=%async_computation.2 | async-start | bytes 2621440 | tf_op jit(solution)/shard_map/all_gather | solution.py:25
  94.9 2.4 copy-start.5
  94.9 3.6 copy-start.4
  96.3 210.6 %all-gather.5.cloned.1.call-start = ((), (), s32[]{:S(2)}) async-start(), calls=%async_computation.3 | async-start | bytes 36864000 | tf_op jit(solution)/shard_map/all_gather | solution.py:29
  97.1 308.9 %reduce-scatter.2.cloned.1.call-start = ((), (), s32[]{:S(2)}) async-start(), calls=%async_computation.4 | async-start | bytes 2621440 | tf_op jit(solution)/shard_map/reduce_scatter | solution.py:47
  360.5 83.3 %all-reduce.5.cloned.1.call-start = ((), (), s32[]{:S(2)}) async-start(), calls=%async_computation.5 | async-start | bytes 131072 | tf_op jit(solution)/shard_map/psum | solution.py:59
  406.0 2.3 copy-start.1
  411.8 89.1 %all-reduce.7.cloned.1.call-start = ((), (), s32[]{:S(2)}) async-start(), calls=%async_computation.6 | async-start | bytes 131072 | tf_op jit(solution)/shard_map/psum | solution.py:59
Sparse Core Ops, SparseCore 0:
  96.4 45.3 all-gather.2
  143.6 163.2 all-gather.4
  360.7 45.2 reduce-scatter.1
  411.9 31.8 all-reduce.4
  446.7 54.1 all-reduce.6
